TPU v7x, 32 devices: a whole 2x2x4 slice. The times are simulated.
32 devices in a mesh: gx: 8 (over z, y), gy: 4 (over x, core).
Axes of the slice: x: 2, y: 2, z: 4, core: 2. Of those that a mesh axis runs over, the one named last changes fastest.
Arguments:
- vectors: float32 [64, 32768], P(None, ('gx', 'gy')), may hold values from -6 to 6
- tiles: bfloat16 [4096, 256, 256], P(('gx', 'gy')), may hold values from -0.09375 to 0.09375
- counts: int32 [128], P(('gx', 'gy')), may hold values from 1 to 32, 2112 in all
- tile_col: int32 [4096], P(('gx', 'gy')), may hold values from 0 to 31
- send_list: int32 [32, 32, 1], replicated, may hold values from 0 to 3
Outputs:
- basis: float32 [64, 32768], P(None, ('gx', 'gy'))
- rayleigh: float32 [2, 64, 64], replicated
Inputs may be any that keep to these rules, and one draw needn't show every extreme that they name: The first counts[b] of row block b's 32 slots hold its tiles, the others are ignored.
All inputs are finite; a program needn't handle non-finite values.
Results may differ from a plain program's by a relative error of at most 0.0046.
Values may be sent and summed in bfloat16 or wider, within the bound.
No kernel may reach another device: no remote copies, remote signals or barrier semaphores. Data moves between devices by JAX's collectives and lax.ppermute only.
A program may use at most 64 MiB of HBM per device.

v0:
```python
import jax
import jax.numpy as jnp
from jax import lax
from jax.sharding import PartitionSpec as P

ITERS = 2


def on_device(vectors, tiles, counts, tile_col, send_list):
    me = lax.axis_index(("gx", "gy"))
    devices = lax.axis_size(("gx", "gy"))
    rows_here = vectors.shape[1]
    blocks_here = counts.shape[0]
    tile_size = tiles.shape[1]
    depth = tiles.shape[0] // blocks_here
    width = vectors.shape[0]
    total_rows = rows_here * devices
    live = (jnp.arange(tiles.shape[0], dtype=jnp.int32) % depth < jnp.repeat(counts, depth)).astype(
        jnp.float32
    )
    outgoing = lax.dynamic_index_in_dim(send_list, me, 0, keepdims=False).reshape(-1)
    current = vectors
    rayleigh = []
    for step in range(ITERS):
        rounded = current.astype(jnp.bfloat16)
        own_blocks = rounded.reshape(width, blocks_here, tile_size).transpose(1, 0, 2)
        parcel = jnp.take(own_blocks, outgoing, axis=0)
        arrived = lax.all_to_all(parcel, ("gx", "gy"), split_axis=0, concat_axis=0, tiled=True)
        picked = jnp.take(arrived, tile_col, axis=0)
        prod = jnp.einsum("jrc,jkc->jkr", tiles, picked, preferred_element_type=jnp.float32)
        prod = prod * live[:, None, None]
        image = prod.reshape(blocks_here, depth, width, tile_size).sum(axis=1)
        image = image.transpose(1, 0, 2).reshape(width, rows_here)
        gram_part = jnp.dot(image, image.T, precision=lax.Precision.HIGHEST)
        quotient_part = jnp.dot(current, image.T, precision=lax.Precision.HIGHEST)
        gram, quotient = lax.psum((gram_part, quotient_part), ("gx", "gy"))
        gram = gram / total_rows
        rayleigh.append(quotient / jnp.sqrt(jnp.float32(total_rows)))
        lower = jnp.linalg.cholesky(gram)
        current = lax.linalg.triangular_solve(lower, image, left_side=True, lower=True)
    return (current, jnp.stack(rayleigh))


def solution(mesh):
    return jax.shard_map(
        on_device,
        mesh=mesh,
        in_specs=(
            P(None, ("gx", "gy")),
            P(("gx", "gy"), None, None),
            P(("gx", "gy")),
            P(("gx", "gy")),
            P(),
        ),
        out_specs=(P(None, ("gx", "gy")), P()),
        check_vma=False,
    )
```

profile of v0, /device:TPU:0, one launch (start us, length us, event | category | flops | bytes accessed | tf_op | source)
XLA Modules:
  0.0 203.6 jit_solution(17290401623316212389)
XLA Ops:
  0.6 0.0 copy-start.1
  0.6 0.0 copy-start.2
  0.7 0.7 compare_and_fusion.1
  1.3 1.0 convert_element_type.13
  2.3 0.6 gather_fusion
  2.9 1.2 broadcast_select_fusion
  4.1 7.3 %all-to-all-start = ((bf16[32,64,256]{2,1,0:T(8,128)(2,1)}), bf16[32,64,256]{2,1,0:T(8,128)(2,1)S(1)}, u32[]{:S(2)}, u32[]{:S(2)}) async-start(bf16[32,64,256]{2,1,0:T(8,128)(2,1)} %broadcast_select_fusion), calls=%async_computation | async-start | bytes 2097152 | tf_op jit(solution)/shard_map/all_to_all | solution.py:28
  11.4 0.0 copy-done.1
  11.4 0.1 broadcast_in_dim.24
  11.5 0.1 reshape.67
  11.6 0.0 copy-done.2
  11.6 26.0 %all-to-all-done = bf16[32,64,256]{2,1,0:T(8,128)(2,1)S(1)} async-done(((bf16[32,64,256]{2,1,0:T(8,128)(2,1)}), bf16[32,64,256]{2,1,0:T(8,128)(2,1)S(1)}, u32[]{:S(2)}, u32[]{:S(2)}) %all-to-all-start) | async-done | bytes 1048608 | tf_op jit(solution)/shard_map/all_to_all | solution.py:28
  37.6 2.7 %gather_fusion.1 = bf16[128,64,256]{2,1,0:T(8,128)(2,1)} fusion(bf16[32,64,256]{2,1,0:T(8,128)(2,1)S(1)} %all-to-all-done, s32[1024]{0:T(1024)S(1)} %pad_clamp_fusion), kind=kCustom, calls=%fused_computation.1.clone | custom fusion | bytes 8389120 | tf_op jit(solution)/shard_map/jit(_take)/gather | solution.py:29
  40.4 10.9 %bitcast_reduce_fusion.1 = f32[4,64,256]{2,1,0:T(8,128)S(1)} fusion(f32[128]{0:T(128)S(1)} %get-tuple-element.22, bf16[128,256,256]{2,1,0:T(8,128)(2,1)} %param.13, bf16[128,64,256]{2,1,0:T(8,128)(2,1)} %gather_fusion.1, pred[128]{0:T(512)(128)(4,1)S(1)} %get-tuple-element.21), kind=kOutput, calls=%fused_computation.5 | convolution fusion | flops 1079967744 | bytes 21234304 | tf_op jit(solution)/shard_map/jrc,jkc->jkr/dot_general | solution.py:30
  51.3 0.0 copy-start
  51.3 0.4 convolution_bitcast_fusion.2
  51.6 38.7 %psum.28 = f32[64,64]{0,1:T(8,128)S(1)} all-reduce(f32[64,64]{0,1:T(8,128)S(1)} %convolution_bitcast_fusion.2), channel_id=1, replica_groups=mesh['gx'=8,'gy'=4] {'gx','gy'}, use_global_device_ids=true, to_apply=%region_1.4 | all-reduce | flops 4096 | bytes 32768 | tf_op jit(solution)/shard_map/psum | solution.py:36
  90.3 0.1 copy.38
  90.4 5.8 %cholesky.44 = f32[64,64]{1,0:T(8,128)S(1)} custom-call(f32[64,64]{1,0:T(8,128)S(1)} %fusion.17), custom_call_target="Cholesky" | custom-call | tf_op jit(solution)/shard_map/jit(cholesky)/cholesky | solution.py:39
  96.3 0.6 compare_reduce_fusion.1
  97.0 0.7 fusion.10
  97.6 4.9 %custom-call.6 = f32[1,64,64]{1,2,0:T(8,128)S(1)} custom-call(f32[1,64,64]{2,1,0:T(8,128)S(1)} %fusion.10), custom_call_target="InvertDiagBlocksLowerTriangular" | custom-call | tf_op jit(solution)/shard_map/triangular_solve/custom-call.0 | solution.py:40
  102.6 0.4 fusion.22
  103.0 0.6 gather_fusion.2
  103.6 1.2 broadcast_select_fusion.1
  104.8 4.4 %all-to-all-start.1 = ((bf16[32,64,256]{2,1,0:T(8,128)(2,1)}), bf16[32,64,256]{2,1,0:T(8,128)(2,1)S(1)}, u32[]{:S(2)}, u32[]{:S(2)}) async-start(bf16[32,64,256]{2,1,0:T(8,128)(2,1)} %broadcast_select_fusion.1), calls=%async_computation.1 | async-start | bytes 2097152 | tf_op jit(solution)/shard_map/all_to_all | solution.py:28
  109.1 0.0 copy-done
  109.1 0.4 convolution_bitcast_fusion
  109.5 25.8 %all-to-all-done.1 = bf16[32,64,256]{2,1,0:T(8,128)(2,1)S(1)} async-done(((bf16[32,64,256]{2,1,0:T(8,128)(2,1)}), bf16[32,64,256]{2,1,0:T(8,128)(2,1)S(1)}, u32[]{:S(2)}, u32[]{:S(2)}) %all-to-all-start.1) | async-done | bytes 1048608 | tf_op jit(solution)/shard_map/all_to_all | solution.py:28
  135.3 2.7 %gather_fusion.3 = bf16[128,64,256]{2,1,0:T(8,128)(2,1)} fusion(bf16[32,64,256]{2,1,0:T(8,128)(2,1)S(1)} %all-to-all-done.1, s32[1024]{0:T(1024)S(1)} %pad_clamp_fusion), kind=kCustom, calls=%fused_computation.3.clone | custom fusion | bytes 8389120 | tf_op jit(solution)/shard_map/jit(_take)/gather | solution.py:29
  138.1 10.9 %bitcast_reduce_fusion = f32[4,64,256]{2,1,0:T(8,128)S(1)} fusion(f32[128]{0:T(128)S(1)} %get-tuple-element.22, bf16[128,256,256]{2,1,0:T(8,128)(2,1)} %param.13, bf16[128,64,256]{2,1,0:T(8,128)(2,1)} %gather_fusion.3, pred[128]{0:T(512)(128)(4,1)S(1)} %get-tuple-element.21), kind=kOutput, calls=%fused_computation.4 | convolution fusion | flops 1079967744 | bytes 21234304 | tf_op jit(solution)/shard_map/jrc,jkc->jkr/dot_general | solution.py:30
  149.0 0.4 convolution_bitcast_fusion.1
  149.4 0.4 fusion.23
  149.7 39.8 %all-reduce = (f32[64,64]{0,1:T(8,128)S(1)}, f32[64,64]{0,1:T(8,128)S(1)}, f32[64,64]{0,1:T(8,128)S(1)}) all-reduce(f32[64,64]{0,1:T(8,128)S(1)} %convolution_bitcast_fusion.1, f32[64,64]{0,1:T(8,128)S(1)} %fusion.23, f32[64,64]{0,1:T(8,128)S(1)} %convolution_bitcast_fusion), channel_id=1, replica_groups=mesh['gx'=8,'gy'=4] {'gx','gy'}, use_global_device_ids=true, to_apply=%region_5.10 | all-reduce | flops 12288 | bytes 98304 | tf_op jit(solution)/shard_map/psum | solution.py:36
  189.6 0.7 copy.45
  190.3 0.1 copy.42
  190.4 5.8 %cholesky.55 = f32[64,64]{1,0:T(8,128)S(1)} custom-call(f32[64,64]{1,0:T(8,128)S(1)} %fusion.14), custom_call_target="Cholesky" | custom-call | tf_op jit(solution)/shard_map/jit(cholesky)/cholesky | solution.py:39
  196.3 0.6 compare_reduce_fusion
  196.9 0.7 fusion.11
  197.6 4.9 %custom-call.7 = f32[1,64,64]{1,2,0:T(8,128)S(1)} custom-call(f32[1,64,64]{2,1,0:T(8,128)S(1)} %fusion.11), custom_call_target="InvertDiagBlocksLowerTriangular" | custom-call | tf_op jit(solution)/shard_map/triangular_solve/custom-call.0 | solution.py:40
  202.5 1.1 fusion.12
  (17 shorter events, 0.2 us)
Async XLA Ops:
  0.6 10.8 %copy-start.1 = (s32[4]{0:T(128)S(1)}, s32[4]{0:T(128)}, u32[]{:S(2)}) copy-start(s32[4]{0:T(128)} %param.14) | copy-start | bytes 52
  0.6 11.0 %copy-start.2 = (s32[128]{0:T(128)S(1)}, s32[128]{0:T(128)}, u32[]{:S(2)}) copy-start(s32[128]{0:T(128)} %param.15) | copy-start | bytes 1540
  4.1 33.5 %all-to-all-start = ((bf16[32,64,256]{2,1,0:T(8,128)(2,1)}), bf16[32,64,256]{2,1,0:T(8,128)(2,1)S(1)}, u32[]{:S(2)}, u32[]{:S(2)}) async-start(bf16[32,64,256]{2,1,0:T(8,128)(2,1)} %broadcast_select_fusion), calls=%async_computation | async-start | bytes 2097152 | tf_op jit(solution)/shard_map/all_to_all | solution.py:28
  51.3 57.9 %copy-start = (f32[64,1024]{1,0:T(8,128)S(1)}, f32[64,1024]{1,0:T(8,128)}, u32[]{:S(2)}) copy-start(f32[64,1024]{1,0:T(8,128)} %param.12) | copy-start | bytes 786436
  104.8 30.6 %all-to-all-start.1 = ((bf16[32,64,256]{2,1,0:T(8,128)(2,1)}), bf16[32,64,256]{2,1,0:T(8,128)(2,1)S(1)}, u32[]{:S(2)}, u32[]{:S(2)}) async-start(bf16[32,64,256]{2,1,0:T(8,128)(2,1)} %broadcast_select_fusion.1), calls=%async_computation.1 | async-start | bytes 2097152 | tf_op jit(solution)/shard_map/all_to_all | solution.py:28
where the time goes:
time: 204 us
  blocking collectives  78.5 us (38%)
  waiting for transfers between devices  51.8 us (25%)
  other arithmetic  28.2 us (14%)
  matrix products  24.8 us (12%)
  starting transfers between devices  11.7 us (6%)
  local copies, waits for them, and re-layouts  7.81 us (4%)
    psum x2, blocking collectives, on_device(): gram, quotient = lax.psum((gram_part, quotient_part), ('gx', 'gy'))  78.5 us
    all_to_all x2, waiting for transfers between devices, on_device(): lax.all_to_all(parcel, ('gx', 'gy'), split_axis=0, concat_axis=0, tiled=T...  51.8 us
    dot_general x2, matrix products, on_device(): jnp.einsum('jrc,jkc->jkr', tiles, picked, preferred_element_type=jnp.floa...  21.8 us
    another operation x6, other arithmetic, on_device(): lower = jnp.linalg.cholesky(gram)  13 us
    all_to_all x2, starting transfers between devices, on_device(): lax.all_to_all(parcel, ('gx', 'gy'), split_axis=0, concat_axis=0, tiled=T...  11.7 us
    another operation x4, other arithmetic, on_device(): lax.linalg.triangular_solve(lower, image, left_side=True, lower=True)  11.1 us
    gather x2, local copies, waits for them, and re-layouts, on_device(): picked = jnp.take(arrived, tile_col, axis=0)  5.48 us
  transfers between devices with their start and end apart: 2, of which 2 were waited for; matrix products, arithmetic and copies ran while one was open for 0% of the time, Pallas kernels for 0%

commit v1 on v0

--- a/solution.py
+++ b/solution.py
@@ -33,7 +33,7 @@
         image = image.transpose(1, 0, 2).reshape(width, rows_here)
         gram_part = jnp.dot(image, image.T, precision=lax.Precision.HIGHEST)
         quotient_part = jnp.dot(current, image.T, precision=lax.Precision.HIGHEST)
-        gram, quotient = lax.psum((gram_part, quotient_part), ("gx", "gy"))
+        gram, quotient = lax.psum(lax.psum((gram_part, quotient_part), "gy"), "gx")
         gram = gram / total_rows
         rayleigh.append(quotient / jnp.sqrt(jnp.float32(total_rows)))
         lower = jnp.linalg.cholesky(gram)

time: 204 us -> 219 us (1.074)
  blocking collectives: 78.5 us -> 95 us
    psum x2 -> x4, blocking collectives: 78.5 us -> 95 us  [on_device(): gram, quotient = lax.psum(lax.psum((gram_part, quotient_part), 'gy'), 'gx')]
where the time goes in v1:
time: 219 us; the launch traced here: 218 us
  blocking collectives  95 us (43%)
  waiting for transfers between devices  51.8 us (24%)
  other arithmetic  28.2 us (13%)
  matrix products  24.8 us (11%)
  starting transfers between devices  9.97 us (5%)
  local copies, waits for them, and re-layouts  7.81 us (4%)
    psum x4, blocking collectives, on_device(): gram, quotient = lax.psum(lax.psum((gram_part, quotient_part), 'gy'), 'gx')  95 us
    all_to_all x2, waiting for transfers between devices, on_device(): lax.all_to_all(parcel, ('gx', 'gy'), split_axis=0, concat_axis=0, tiled=T...  51.8 us
    dot_general x2, matrix products, on_device(): jnp.einsum('jrc,jkc->jkr', tiles, picked, preferred_element_type=jnp.floa...  21.8 us
    another operation x6, other arithmetic, on_device(): lower = jnp.linalg.cholesky(gram)  13 us
    another operation x4, other arithmetic, on_device(): lax.linalg.triangular_solve(lower, image, left_side=True, lower=True)  11.1 us
    all_to_all x2, starting transfers between devices, on_device(): lax.all_to_all(parcel, ('gx', 'gy'), split_axis=0, concat_axis=0, tiled=T...  9.97 us
    gather x2, local copies, waits for them, and re-layouts, on_device(): picked = jnp.take(arrived, tile_col, axis=0)  5.48 us
  transfers between devices with their start and end apart: 2, of which 2 were waited for; matrix products, arithmetic and copies ran while one was open for 0% of the time, Pallas kernels for 0%

profile of v1, /device:TPU:0, one launch (start us, length us, event | category | flops | bytes accessed | tf_op | source)
XLA Modules:
  0.0 218.5 jit_solution(273658512589877633)
XLA Ops:
  0.6 0.0 copy-start.1
  0.6 0.0 copy-start.2
  0.7 0.7 compare_and_fusion.1
  1.3 1.0 convert_element_type.13
  2.3 0.6 gather_fusion
  2.9 1.2 broadcast_select_fusion
  4.1 7.3 %all-to-all-start = ((bf16[32,64,256]{2,1,0:T(8,128)(2,1)}), bf16[32,64,256]{2,1,0:T(8,128)(2,1)S(1)}, u32[]{:S(2)}, u32[]{:S(2)}) async-start(bf16[32,64,256]{2,1,0:T(8,128)(2,1)} %broadcast_select_fusion), calls=%async_computation | async-start | bytes 2097152 | tf_op jit(solution)/shard_map/all_to_all | solution.py:28
  11.4 0.0 copy-done.1
  11.4 0.1 broadcast_in_dim.24
  11.5 0.1 reshape.67
  11.6 0.0 copy-done.2
  11.6 26.0 %all-to-all-done = bf16[32,64,256]{2,1,0:T(8,128)(2,1)S(1)} async-done(((bf16[32,64,256]{2,1,0:T(8,128)(2,1)}), bf16[32,64,256]{2,1,0:T(8,128)(2,1)S(1)}, u32[]{:S(2)}, u32[]{:S(2)}) %all-to-all-start) | async-done | bytes 1048608 | tf_op jit(solution)/shard_map/all_to_all | solution.py:28
  37.6 2.7 %gather_fusion.1 = bf16[128,64,256]{2,1,0:T(8,128)(2,1)} fusion(bf16[32,64,256]{2,1,0:T(8,128)(2,1)S(1)} %all-to-all-done, s32[1024]{0:T(1024)S(1)} %pad_clamp_fusion), kind=kCustom, calls=%fused_computation.1.clone | custom fusion | bytes 8389120 | tf_op jit(solution)/shard_map/jit(_take)/gather | solution.py:29
  40.4 10.9 %bitcast_reduce_fusion.1 = f32[4,64,256]{2,1,0:T(8,128)S(1)} fusion(f32[128]{0:T(128)S(1)} %get-tuple-element.25, bf16[128,256,256]{2,1,0:T(8,128)(2,1)} %param.13, bf16[128,64,256]{2,1,0:T(8,128)(2,1)} %gather_fusion.1, pred[128]{0:T(512)(128)(4,1)S(1)} %get-tuple-element.24), kind=kOutput, calls=%fused_computation.5 | convolution fusion | flops 1079967744 | bytes 21234304 | tf_op jit(solution)/shard_map/jrc,jkc->jkr/dot_general | solution.py:30
  51.3 0.4 convolution_bitcast_fusion.2
  51.6 0.0 copy-start
  51.6 11.5 %psum.56 = f32[64,64]{0,1:T(8,128)S(1)} all-reduce(f32[64,64]{0,1:T(8,128)S(1)} %convolution_bitcast_fusion.2), channel_id=1, replica_groups=mesh['gx'=8,'gy'=4] {'gy'}, use_global_device_ids=true, to_apply=%region_1.4 | all-reduce | flops 4096 | bytes 32768 | tf_op jit(solution)/shard_map/psum | solution.py:36
  63.1 35.2 %psum.57 = f32[64,64]{0,1:T(8,128)S(1)} all-reduce(f32[64,64]{0,1:T(8,128)S(1)} %psum.56), channel_id=1, replica_groups=mesh['gx'=8,'gy'=4] {'gx'}, use_global_device_ids=true, to_apply=%region_2.5 | all-reduce | flops 4096 | bytes 32768 | tf_op jit(solution)/shard_map/psum | solution.py:36
  98.3 0.1 copy.38
  98.4 5.8 %cholesky.44 = f32[64,64]{1,0:T(8,128)S(1)} custom-call(f32[64,64]{1,0:T(8,128)S(1)} %fusion.17), custom_call_target="Cholesky" | custom-call | tf_op jit(solution)/shard_map/jit(cholesky)/cholesky | solution.py:39
  104.3 0.6 compare_reduce_fusion.1
  104.9 0.7 fusion.10
  105.6 4.9 %custom-call.6 = f32[1,64,64]{1,2,0:T(8,128)S(1)} custom-call(f32[1,64,64]{2,1,0:T(8,128)S(1)} %fusion.10), custom_call_target="InvertDiagBlocksLowerTriangular" | custom-call | tf_op jit(solution)/shard_map/triangular_solve/custom-call.0 | solution.py:40
  110.5 0.4 fusion.22
  111.0 0.6 gather_fusion.2
  111.6 1.2 broadcast_select_fusion.1
  112.8 2.6 %all-to-all-start.1 = ((bf16[32,64,256]{2,1,0:T(8,128)(2,1)}), bf16[32,64,256]{2,1,0:T(8,128)(2,1)S(1)}, u32[]{:S(2)}, u32[]{:S(2)}) async-start(bf16[32,64,256]{2,1,0:T(8,128)(2,1)} %broadcast_select_fusion.1), calls=%async_computation.1 | async-start | bytes 2097152 | tf_op jit(solution)/shard_map/all_to_all | solution.py:28
  115.4 0.0 copy-done
  115.4 0.4 convolution_bitcast_fusion
  115.8 25.8 %all-to-all-done.1 = bf16[32,64,256]{2,1,0:T(8,128)(2,1)S(1)} async-done(((bf16[32,64,256]{2,1,0:T(8,128)(2,1)}), bf16[32,64,256]{2,1,0:T(8,128)(2,1)S(1)}, u32[]{:S(2)}, u32[]{:S(2)}) %all-to-all-start.1) | async-done | bytes 1048608 | tf_op jit(solution)/shard_map/all_to_all | solution.py:28
  141.6 2.7 %gather_fusion.3 = bf16[128,64,256]{2,1,0:T(8,128)(2,1)} fusion(bf16[32,64,256]{2,1,0:T(8,128)(2,1)S(1)} %all-to-all-done.1, s32[1024]{0:T(1024)S(1)} %pad_clamp_fusion), kind=kCustom, calls=%fused_computation.3.clone | custom fusion | bytes 8389120 | tf_op jit(solution)/shard_map/jit(_take)/gather | solution.py:29
  144.3 10.9 %bitcast_reduce_fusion = f32[4,64,256]{2,1,0:T(8,128)S(1)} fusion(f32[128]{0:T(128)S(1)} %get-tuple-element.25, bf16[128,256,256]{2,1,0:T(8,128)(2,1)} %param.13, bf16[128,64,256]{2,1,0:T(8,128)(2,1)} %gather_fusion.3, pred[128]{0:T(512)(128)(4,1)S(1)} %get-tuple-element.24), kind=kOutput, calls=%fused_computation.4 | convolution fusion | flops 1079967744 | bytes 21234304 | tf_op jit(solution)/shard_map/jrc,jkc->jkr/dot_general | solution.py:30
  155.2 0.4 convolution_bitcast_fusion.1
  155.6 0.4 fusion.23
  156.0 12.4 %all-reduce.1 = (f32[64,64]{0,1:T(8,128)S(1)}, f32[64,64]{0,1:T(8,128)S(1)}, f32[64,64]{0,1:T(8,128)S(1)}) all-reduce(f32[64,64]{0,1:T(8,128)S(1)} %convolution_bitcast_fusion.1, f32[64,64]{0,1:T(8,128)S(1)} %fusion.23, f32[64,64]{0,1:T(8,128)S(1)} %convolution_bitcast_fusion), channel_id=1, replica_groups=mesh['gx'=8,'gy'=4] {'gy'}, use_global_device_ids=true, to_apply=%region_6.11 | all-reduce | flops 12288 | bytes 98304 | tf_op jit(solution)/shard_map/psum | solution.py:36
  168.4 36.0 %all-reduce = (f32[64,64]{0,1:T(8,128)S(1)}, f32[64,64]{0,1:T(8,128)S(1)}, f32[64,64]{0,1:T(8,128)S(1)}) all-reduce(f32[64,64]{0,1:T(8,128)S(1)} %get-tuple-element.17, f32[64,64]{0,1:T(8,128)S(1)} %get-tuple-element.18, f32[64,64]{0,1:T(8,128)S(1)} %get-tuple-element.19), channel_id=1, replica_groups=mesh['gx'=8,'gy'=4] {'gx'}, use_global_device_ids=true, to_apply=%region_7.12 | all-reduce | flops 12288 | bytes 98304 | tf_op jit(solution)/shard_map/psum | solution.py:36
  204.4 0.7 copy.45
  205.1 0.1 copy.42
  205.2 5.8 %cholesky.55 = f32[64,64]{1,0:T(8,128)S(1)} custom-call(f32[64,64]{1,0:T(8,128)S(1)} %fusion.14), custom_call_target="Cholesky" | custom-call | tf_op jit(solution)/shard_map/jit(cholesky)/cholesky | solution.py:39
  211.1 0.6 compare_reduce_fusion
  211.8 0.7 fusion.11
  212.4 4.9 %custom-call.7 = f32[1,64,64]{1,2,0:T(8,128)S(1)} custom-call(f32[1,64,64]{2,1,0:T(8,128)S(1)} %fusion.11), custom_call_target="InvertDiagBlocksLowerTriangular" | custom-call | tf_op jit(solution)/shard_map/triangular_solve/custom-call.0 | solution.py:40
  217.3 1.1 fusion.12
  (17 shorter events, 0.2 us)
Async XLA Ops:
  0.6 10.8 %copy-start.1 = (s32[4]{0:T(128)S(1)}, s32[4]{0:T(128)}, u32[]{:S(2)}) copy-start(s32[4]{0:T(128)} %param.14) | copy-start | bytes 52
  0.6 11.0 %copy-start.2 = (s32[128]{0:T(128)S(1)}, s32[128]{0:T(128)}, u32[]{:S(2)}) copy-start(s32[128]{0:T(128)} %param.15) | copy-start | bytes 1540
  4.1 33.5 %all-to-all-start = ((bf16[32,64,256]{2,1,0:T(8,128)(2,1)}), bf16[32,64,256]{2,1,0:T(8,128)(2,1)S(1)}, u32[]{:S(2)}, u32[]{:S(2)}) async-start(bf16[32,64,256]{2,1,0:T(8,128)(2,1)} %broadcast_select_fusion), calls=%async_computation | async-start | bytes 2097152 | tf_op jit(solution)/shard_map/all_to_all | solution.py:28
  51.6 63.8 %copy-start = (f32[64,1024]{1,0:T(8,128)S(1)}, f32[64,1024]{1,0:T(8,128)}, u32[]{:S(2)}) copy-start(f32[64,1024]{1,0:T(8,128)} %param.12) | copy-start | bytes 786436
  112.8 28.8 %all-to-all-start.1 = ((bf16[32,64,256]{2,1,0:T(8,128)(2,1)}), bf16[32,64,256]{2,1,0:T(8,128)(2,1)S(1)}, u32[]{:S(2)}, u32[]{:S(2)}) async-start(bf16[32,64,256]{2,1,0:T(8,128)(2,1)} %broadcast_select_fusion.1), calls=%async_computation.1 | async-start | bytes 2097152 | tf_op jit(solution)/shard_map/all_to_all | solution.py:28
